TPU v7x, 32 devices: a whole 2x2x4 slice. The times are simulated.
32 devices in a mesh: pts: 16 (over z, y, x), grp: 2 (over core).
Axes of the slice: x: 2, y: 2, z: 4, core: 2. Of those that a mesh axis runs over, the one named last changes fastest.
Arguments:
- cam_jac: float32 [18, 262144], P(None, ('pts', 'grp')), may hold values from -0.25 to 0.25
- pt_jac: float32 [6, 262144], P(None, ('pts', 'grp')), may hold values from -6 to 6
- resid: float32 [2, 262144], P(None, ('pts', 'grp')), may hold values from -102 to 102
- obs_point: int32 [262144], P(('pts', 'grp')), may hold values from 0 to 65535, as said below
- obs_camera: int32 [262144], P(('pts', 'grp')), may hold values from 0 to 511
- camera_slot: int32 [512], replicated, may hold values from 0 to 511, each once
Outputs:
- cam_inverse: float32 [81, 512], P(None, ('pts', 'grp'))
- precond: float32 [9, 262144], P(None, ('pts', 'grp'))
Inputs may be any that keep to these rules, and one draw needn't show every extreme that they name: `obs_point`: observation o names a point of block o // 8192, from (o // 8192) * 2048 to (o // 8192 + 1) * 2048 - 1; within each block of 8192 observations the point number never falls and rises by at most 1 from one observation to the next, and the block's first observation names the block's first point. Each slot appears once; camera c is owned by device camera_slot[c] // 16 of the joined axes pts+grp.
All inputs are finite; a program needn't handle non-finite values.
Results may differ from a plain program's by a relative error of at most 0.0003.
Values sent between devices are 32-bit elements; how exact they have to be, the bound alone decides.
A program may use at most 64 MiB of HBM per device.

v0:
```python
import jax
import jax.numpy as jnp
from jax import lax
from jax.sharding import PartitionSpec as P

PTS_DEV = 2048


DAMP = 1.0
SPAN = 512


def lower_pairs():
    return [(row_at, col_at) for row_at in range(9) for col_at in range(row_at + 1)]


def exact_dot(left, right):
    return jnp.dot(left, right, precision=lax.Precision.HIGHEST, preferred_element_type=jnp.float32)


def point_table(pt_jac, resid, local_point, npoints):
    entries = []
    for row_at in range(3):
        for col_at in range(row_at, 3):
            entries.append(
                pt_jac[row_at] * pt_jac[col_at] + pt_jac[3 + row_at] * pt_jac[3 + col_at]
            )
    for row_at in range(3):
        entries.append(pt_jac[row_at] * resid[0] + pt_jac[3 + row_at] * resid[1])
    stacked = jnp.stack(entries, 0)
    count = stacked.shape[1] // SPAN
    pieces = jnp.moveaxis(stacked.reshape(9, count, SPAN), 1, 0)
    point_rows = local_point.reshape(count, SPAN)
    firsts = point_rows[:, 0]
    window_ids = jnp.arange(SPAN, dtype=jnp.int32)

    def add_block(carry, inputs):
        piece, points, first = inputs
        onehot = (points[:, None] - first == window_ids[None, :]).astype(jnp.float32)
        window = lax.dynamic_slice_in_dim(carry, first, SPAN, 1)
        carry = lax.dynamic_update_slice_in_dim(carry, window + exact_dot(piece, onehot), first, 1)
        return (carry, None)

    sums, unused = lax.scan(
        add_block, jnp.zeros((9, npoints + SPAN), jnp.float32), (pieces, point_rows, firsts)
    )
    v00 = sums[0] + DAMP
    v01 = sums[1]
    v02 = sums[2]
    v11 = sums[3] + DAMP
    v12 = sums[4]
    v22 = sums[5] + DAMP
    c00 = v11 * v22 - v12 * v12
    c01 = v02 * v12 - v01 * v22
    c02 = v01 * v12 - v02 * v11
    c11 = v00 * v22 - v02 * v02
    c12 = v01 * v02 - v00 * v12
    c22 = v00 * v11 - v01 * v01
    determ = v00 * c00 + v01 * c01 + v02 * c02
    i00 = c00 / determ
    i01 = c01 / determ
    i02 = c02 / determ
    i11 = c11 / determ
    i12 = c12 / determ
    i22 = c22 / determ
    w_zero = i00 * sums[6] + i01 * sums[7] + i02 * sums[8]
    w_one = i01 * sums[6] + i11 * sums[7] + i12 * sums[8]
    w_two = i02 * sums[6] + i12 * sums[7] + i22 * sums[8]
    table = jnp.stack([i00, i01, i02, i11, i12, i22, w_zero, w_one, w_two], 0)

    def pick_block(carry, inputs):
        points, first = inputs
        onehot = (points[:, None] - first == window_ids[None, :]).astype(jnp.float32)
        window = lax.dynamic_slice_in_dim(table, first, SPAN, 1)
        return (carry, exact_dot(window, onehot.T))

    unused, picked = lax.scan(pick_block, 0, (point_rows, firsts))
    return jnp.moveaxis(picked, 0, 1).reshape(9, count * SPAN)


def obs_terms(cam_jac, pt_jac, resid, point_rows, pairs):
    i00, i01, i02, i11, i12, i22 = [point_rows[pos] for pos in range(6)]
    weights = [point_rows[6], point_rows[7], point_rows[8]]
    vinv = ((i00, i01, i02), (i01, i11, i12), (i02, i12, i22))
    prow = [[pt_jac[3 * rowp + inner] for inner in range(3)] for rowp in range(2)]
    usage = [
        [
            vinv[outer][0] * prow[rowp][0]
            + vinv[outer][1] * prow[rowp][1]
            + vinv[outer][2] * prow[rowp][2]
            for outer in range(3)
        ]
        for rowp in range(2)
    ]
    proj_zz = prow[0][0] * usage[0][0] + prow[0][1] * usage[0][1] + prow[0][2] * usage[0][2]
    proj_zo = prow[0][0] * usage[1][0] + prow[0][1] * usage[1][1] + prow[0][2] * usage[1][2]
    proj_oo = prow[1][0] * usage[1][0] + prow[1][1] * usage[1][1] + prow[1][2] * usage[1][2]
    keep = ((1.0 - proj_zz, -proj_zo), (-proj_zo, 1.0 - proj_oo))
    shifted = [
        resid[rowp]
        - (prow[rowp][0] * weights[0] + prow[rowp][1] * weights[1] + prow[rowp][2] * weights[2])
        for rowp in range(2)
    ]
    reduced = jnp.stack(
        [cam_jac[col_at] * shifted[0] + cam_jac[9 + col_at] * shifted[1] for col_at in range(9)], 0
    )
    mixed = [
        [
            keep[rowp][0] * cam_jac[col_at] + keep[rowp][1] * cam_jac[9 + col_at]
            for col_at in range(9)
        ]
        for rowp in range(2)
    ]
    terms = jnp.stack(
        [
            cam_jac[row_at] * mixed[0][col_at] + cam_jac[9 + row_at] * mixed[1][col_at]
            for row_at, col_at in pairs
        ],
        0,
    )
    return (terms, reduced)


def chol_inverse(rows, pairs):
    entry = {pair: rows[pos] for pos, pair in enumerate(pairs)}
    factor = {}
    for col_at in range(9):
        diag = entry[col_at, col_at] + DAMP
        for inner in range(col_at):
            diag = diag - factor[col_at, inner] * factor[col_at, inner]
        root = jnp.sqrt(diag)
        factor[col_at, col_at] = root
        for row_at in range(col_at + 1, 9):
            value = entry[row_at, col_at]
            for inner in range(col_at):
                value = value - factor[row_at, inner] * factor[col_at, inner]
            factor[row_at, col_at] = value / root
    solved = {}
    for col_at in range(9):
        solved[col_at, col_at] = 1.0 / factor[col_at, col_at]
        for row_at in range(col_at + 1, 9):
            value = factor[row_at, col_at] * solved[col_at, col_at]
            for inner in range(col_at + 1, row_at):
                value = value + factor[row_at, inner] * solved[inner, col_at]
            solved[row_at, col_at] = -value / factor[row_at, row_at]
    result = {}
    for row_at in range(9):
        for col_at in range(row_at + 1):
            value = solved[row_at, row_at] * solved[row_at, col_at]
            for inner in range(row_at + 1, 9):
                value = value + solved[inner, row_at] * solved[inner, col_at]
            result[row_at, col_at] = value
            result[col_at, row_at] = value
    return jnp.stack([result[row_at, col_at] for row_at in range(9) for col_at in range(9)], 0)


def apply_inverse(picked, reduced, locate):
    outputs = []
    for row_at in range(9):
        value = picked[locate[row_at, 0]] * reduced[0]
        for col_at in range(1, 9):
            value = value + picked[locate[row_at, col_at]] * reduced[col_at]
        outputs.append(value)
    return jnp.stack(outputs, 0)


def shards(cam_jac, pt_jac, resid, obs_point, obs_camera, camera_slot):
    cameras = camera_slot.shape[0]
    local_point = obs_point - lax.axis_index(("pts", "grp")) * PTS_DEV
    rows = point_table(pt_jac, resid, local_point, PTS_DEV)
    pairs = lower_pairs()
    terms, reduced = obs_terms(cam_jac, pt_jac, resid, rows, pairs)
    width = len(pairs)
    camera_of_slot = (
        jnp.zeros((cameras,), jnp.int32).at[camera_slot].set(jnp.arange(cameras, dtype=jnp.int32))
    )
    count = terms.shape[1] // SPAN
    term_blocks = jnp.moveaxis(terms.reshape(width, count, SPAN), 1, 0)
    camera_blocks = obs_camera.reshape(count, SPAN)

    def add_cameras(carry, inputs):
        piece, named = inputs
        onehot = (named[:, None] == camera_of_slot[None, :]).astype(jnp.bfloat16)
        return (carry + exact_dot(piece, onehot.astype(jnp.float32)), None)

    partial_value, unused = lax.scan(
        add_cameras, jnp.zeros((width, cameras), jnp.float32), (term_blocks, camera_blocks)
    )
    owned = lax.psum_scatter(partial_value, ("pts", "grp"), scatter_dimension=1, tiled=True)
    inverse = chol_inverse(owned, pairs)
    outgoing = jnp.stack([inverse[row_at * 9 + col_at] for row_at, col_at in pairs], 0)
    table = lax.all_gather(outgoing, ("pts", "grp"), axis=1, tiled=True)

    def pick_cameras(carry, named):
        onehot = (named[:, None] == camera_of_slot[None, :]).astype(jnp.bfloat16)
        return (carry, exact_dot(table, onehot.astype(jnp.float32).T))

    unused, picked = lax.scan(pick_cameras, 0, camera_blocks)
    picked = jnp.moveaxis(picked, 0, 1).reshape(width, count * SPAN)
    position = {pair: pos for pos, pair in enumerate(pairs)}
    locate = {}
    for row_at in range(9):
        for col_at in range(9):
            if (row_at, col_at) in position:
                locate[row_at, col_at] = position[row_at, col_at]
            else:
                locate[row_at, col_at] = position[col_at, row_at]
    precond = apply_inverse(picked, reduced, locate)
    return (inverse, precond)


def solution(mesh):
    in_specs = (
        P(None, ("pts", "grp")),
        P(None, ("pts", "grp")),
        P(None, ("pts", "grp")),
        P(("pts", "grp")),
        P(("pts", "grp")),
        P(),
    )
    out_specs = (P(None, ("pts", "grp")), P(None, ("pts", "grp")))
    return jax.shard_map(shards, mesh=mesh, in_specs=in_specs, out_specs=out_specs, check_vma=False)
```

profile of v0, /device:TPU:0, one launch (start us, length us, event | category | flops | bytes accessed | tf_op | source)
XLA Modules:
  0.0 427.1 jit_solution(14837827144669589391)
XLA Ops:
  8.1 2.2 multiply_add_fusion.87
  10.3 2.2 multiply_add_fusion.82
  12.9 67.0 %while.44 = (s32[]{:T(128)}, f32[9,2560]{1,0:T(8,128)S(1)}, s32[16]{0:T(128)S(1)}, f32[16,9,512]{2,1,0:T(8,128)S(1)}, s32[16,512]{1,0:T(8,128)S(1)}, /*index=5*/s32[]{:T(128)}, s32[]{:T(128)}, s32[]{:T(128)}) while((s32[]{:T(128)}, f32[9,2560]{1,0:T(8,128)S(1)}, s32[16]{0:T(128)S(1)}, f32[16,9,512]{2,1,0:T(8,128)S(1)}, ...), condition=%wide.region_1.2_spmd.clone, body=%wide.region_0.1_spmd.clone.sunk | while | flops 28578820 | bytes 127135 | solution.py:44
  80.4 60.7 %while.45 = (s32[]{:T(128)}, f32[16,9,512]{2,1,0:T(8,128)S(1)}, s32[16]{0:T(128)S(1)}, f32[9,2560]{1,0:T(8,128)S(1)}, s32[16,512]{1,0:T(8,128)S(1)}, /*index=5*/s32[]{:T(128)}, s32[]{:T(128)}, s32[]{:T(128)}) while((s32[]{:T(128)}, f32[16,9,512]{2,1,0:T(8,128)S(1)}, s32[16]{0:T(128)S(1)}, f32[9,2560]{1,0:T(8,128)S(1)}, ...), condition=%wide.region_3.4_spmd.clone, body=%wide.region_2.3_spmd.clone.sunk | while | flops 28574212 | bytes 71835 | solution.py:77
  144.3 2.6 scatter_custom_fusion
  147.3 1.1 multiply_add_fusion.36
  149.7 1.1 multiply_add_fusion.30
  150.8 6.1 %stack.335 = f32[45,16,512]{2,0,1:T(8,128)S(1)} concatenate(f32[1,16,512]{2,0,1:T(1,128)} %bitcast.279, f32[1,16,512]{2,0,1:T(1,128)} %bitcast.278, f32[1,16,512]{2,0,1:T(1,128)S(1)} %bitcast.258, f32[1,16,512]{2,0,1:T(1,128)} %bitcast.277, f32[1,16,512]{2,0,1:T(1,128)S(1)} %bitcast.257, f32[1,16,512]{2,0,1:T(1,128)S(1)} %bitcast.264, f32[1,16,512]{2,0,1:T(1,128)} %bitcast.276, ...), dimensions={0} | concatenate | bytes 2949120 | tf_op jit(solution)/shard_map/stack | solution.py:114
  156.9 43.8 %while.46 = (s32[]{:T(128)}, f32[45,512]{1,0:T(8,128)}, f32[16,45,512]{2,1,0:T(8,128)S(1)}, s32[16,512]{1,0:T(8,128)}, s32[512]{0:T(512)S(1)}, /*index=5*/s32[]{:T(128)}, s32[]{:T(128)}) while((s32[]{:T(128)}, f32[45,512]{1,0:T(8,128)}, f32[16,45,512]{2,1,0:T(8,128)S(1)}, s32[16,512]{1,0:T(8,128)}, s32[512]{0:T(512)S(1)}, ...), condition=%wide.region_6.7_spmd.clone, body=%wide.region_5.6_spmd.clone.sunk | while | flops 141865984 | bytes 290919 | solution.py:186
  157.7 1.2 convolution_add_fusion.5
  159.6 2.1 convolution_add_fusion.5
  162.4 2.1 convolution_add_fusion.5
  165.2 2.1 convolution_add_fusion.5
  168.0 2.1 convolution_add_fusion.5
  170.7 2.1 convolution_add_fusion.5
  173.5 2.1 convolution_add_fusion.5
  176.3 2.1 convolution_add_fusion.5
  179.1 2.1 convolution_add_fusion.5
  181.9 2.1 convolution_add_fusion.5
  184.7 2.1 convolution_add_fusion.5
  187.5 2.1 convolution_add_fusion.5
  190.3 2.1 convolution_add_fusion.5
  193.0 2.1 convolution_add_fusion.5
  195.8 2.1 convolution_add_fusion.5
  198.6 2.1 convolution_add_fusion.5
  200.7 1.7 copy.356
  202.7 138.4 %reduce-scatter.4.cloned.1.call-done = f32[16,45]{1,0:T(8,128)} async-done(((f32[512,45]{1,0:T(8,128)}), f32[16,45]{1,0:T(8,128)}) %reduce-scatter.4.cloned.1.call-update) | async-done | bytes 2896
  342.1 1.5 fusion.61
  343.6 1.5 fusion.60
  354.2 37.2 %all_gather.3 = f32[45,512]{0,1:T(8,128)S(1)} all-gather(f32[45,16]{0,1:T(8,128)S(1)} %stack.337), channel_id=1, replica_groups=mesh['pts'=16,'grp'=2] {'pts','grp'}, dimensions={1}, use_global_device_ids=true | all-gather | bytes 95040 | tf_op jit(solution)/shard_map/all_gather | solution.py:192
  391.6 23.0 %while.43 = (s32[]{:T(128)}, f32[16,45,512]{2,1,0:T(8,128)S(1)}, s32[16,512]{1,0:T(8,128)}, s32[512]{0:T(512)S(1)}, f32[45,512]{1,0:T(8,128)S(1)}, /*index=5*/s32[]{:T(128)}) while((s32[]{:T(128)}, f32[16,45,512]{2,1,0:T(8,128)S(1)}, s32[16,512]{1,0:T(8,128)}, s32[512]{0:T(512)S(1)}, f32[45,512]{1,0:T(8,128)S(1)}, /*index=5*/s32[]{:T(128)}) %tuple.424), condition=%wide.region_9.10_spmd, body=%wide.region_8.9_spmd.sunk | while | flops 141819904 | bytes 204885 | solution.py:198
  418.4 1.8 stack.338
  (324 shorter events, 122.2 us)
Async XLA Ops:
  7.2 333.9 %reduce-scatter.4.cloned.1.call-start = ((), (), s32[]{:S(2)}) async-start(), calls=%async_computation.1 | async-start | bytes 270336
  80.0 62.0 %copy-start = (f32[18,8192]{1,0:T(8,128)S(1)}, f32[18,8192]{1,0:T(8,128)}, u32[]{:S(2)}) copy-start(f32[18,8192]{1,0:T(8,128)} %param.14) | copy-start | bytes 1769476
  80.0 62.0 %copy-start.1 = (f32[6,8192]{1,0:T(8,128)S(1)}, f32[6,8192]{1,0:T(8,128)}, u32[]{:S(2)}) copy-start(f32[6,8192]{1,0:T(8,128)} %param.15) | copy-start | bytes 589828
  141.1 2.5 copy-start.7
  141.1 2.5 copy-start.6
  156.9 45.6 %copy-start.2 = (f32[2,8192]{1,0:T(2,128)S(1)}, f32[2,8192]{1,0:T(2,128)}, u32[]{:S(2)}) copy-start(f32[2,8192]{1,0:T(2,128)} %param.16) | copy-start | bytes 196612
  156.9 45.6 %copy-start.3 = (f32[1,16,512]{2,0,1:T(1,128)S(1)}, f32[1,16,512]{2,0,1:T(1,128)}, u32[]{:S(2)}) copy-start(f32[1,16,512]{2,0,1:T(1,128)} %get-tuple-element.480) | copy-start | bytes 98308
  156.9 45.6 %copy-start.4 = (f32[1,16,512]{2,0,1:T(1,128)S(1)}, f32[1,16,512]{2,0,1:T(1,128)}, u32[]{:S(2)}) copy-start(f32[1,16,512]{2,0,1:T(1,128)} %get-tuple-element.481) | copy-start | bytes 98308
  156.9 45.6 %copy-start.5 = (f32[1,16,512]{2,0,1:T(1,128)S(1)}, f32[1,16,512]{2,0,1:T(1,128)}, u32[]{:S(2)}) copy-start(f32[1,16,512]{2,0,1:T(1,128)} %get-tuple-element.482) | copy-start | bytes 98308
Sparse Core Ops, SparseCore 0:
  202.6 138.4 reduce-scatter.3
where the time goes:
time: 432 us; the launch traced here: 427 us
  waiting for transfers between devices  138 us (32%)
  local copies, waits for them, and re-layouts  81 us (19%)
  loops' own time  60.8 us (14%)
  matrix products  60.8 us (14%)
  blocking collectives  37.2 us (9%)
  other arithmetic  34.4 us (8%)
  between operations  14.5 us (3%)
    unnamed x2, waiting for transfers between devices  138 us
    dot_general x64, matrix products, exact_dot(): jnp.dot(left, right, precision=lax.Precision.HIGHEST, preferred_element_t...  60.8 us
    dynamic_slice x64, local copies, waits for them, and re-layouts, point_table(): lax.scan(add_block, jnp.zeros((9, npoints + SPAN), jnp.float32), (pieces,...  43.9 us
    all_gather x1, blocking collectives, shards(): table = lax.all_gather(outgoing, ('pts', 'grp'), axis=1, tiled=True)  37.2 us
    another operation x1, loops' own time, point_table(): lax.scan(add_block, jnp.zeros((9, npoints + SPAN), jnp.float32), (pieces,...  30.4 us
    another operation x1, loops' own time, point_table(): unused, picked = lax.scan(pick_block, 0, (point_rows, firsts))  30 us
    sub x16, other arithmetic, pick_block(): points[:, None] - first == window_ids[None, :]  10.1 us
    sub x16, other arithmetic, add_block(): points[:, None] - first == window_ids[None, :]  10.1 us
  transfers between devices with their start and end apart: 1, of which 1 were waited for; matrix products, arithmetic and copies ran while one was open for 0% of the time, Pallas kernels for 0%

commit v1 on v0

v1 whole, which is shorter than its diff:
```python
import functools

import jax
import jax.numpy as jnp
from jax import lax
from jax.experimental import pallas as pl
from jax.experimental.pallas import tpu as pltpu
from jax.sharding import PartitionSpec as P

DAMP = 1.0
LANES = 128
HALF = 64
WIDTH = 48
GROUP = 8 * LANES
CHUNK = 512
PAIRS = [(row_at, col_at) for row_at in range(9) for col_at in range(row_at + 1)]
POSITION = {pair: pos for pos, pair in enumerate(PAIRS)}
VMEM_LIMIT = 48 * 1024 * 1024


def lane_ids(shape):
    return lax.broadcasted_iota(jnp.int32, shape, 1)


def camera_of_slots(slot_ref, cof_ref):
    slots = cof_ref.shape[0]
    block = min(slots, 512)

    def one(step, unused):
        base = pl.multiple_of(step * block, block)
        ids = lax.broadcasted_iota(jnp.int32, (block, LANES), 0) + base
        total = jnp.zeros((block, LANES), jnp.float32)
        for part in range(slot_ref.shape[0]):
            named = lax.broadcasted_iota(jnp.int32, (block, LANES), 1) + part * LANES
            hit = slot_ref[part : part + 1, :] == ids
            total = total + jnp.where(hit, named.astype(jnp.float32), 0.0)
        camera = jnp.sum(total, axis=1, keepdims=True)
        cof_ref[pl.ds(base, block), :] = jnp.broadcast_to(camera, (block, LANES)).astype(jnp.int32)
        return unused

    lax.fori_loop(0, slots // block, one, 0)


def onehot_chunk(cof_ref, camera_ref, first, count):
    pieces = []
    for inner in range(count):
        named = camera_ref[pl.ds(first + inner, 1), :]
        pieces.append(jnp.where(cof_ref[...] == named, 1.0, 0.0).astype(jnp.bfloat16))
    return jnp.concatenate(pieces, axis=1)


def split_rows(value):
    high = value.astype(jnp.bfloat16)
    return high, (value - high.astype(jnp.float32)).astype(jnp.bfloat16)


def local_kernel(
    cam_ref, pt_ref, res_ref, point_ref, camera_ref, slot_ref,
    part_ref, red_ref,
    camf, ptf, xs, ends, keys, fixed, terms, wide, cof, acc,
):
    rows = point_ref.shape[0]
    groups = rows // 8

    def flatten(tile, unused):
        lanes = pl.ds(pl.multiple_of(tile * LANES, LANES), LANES)
        camf[pl.ds(tile * 24, 8), :] = cam_ref[0:8, lanes]
        camf[pl.ds(tile * 24 + 8, 8), :] = cam_ref[8:16, lanes]
        camf[pl.ds(tile * 24 + 16, 2), :] = cam_ref[16:18, lanes]
        ptf[pl.ds(tile * 8, 6), :] = pt_ref[:, lanes]
        ptf[pl.ds(tile * 8 + 6, 2), :] = res_ref[:, lanes]
        return unused

    lax.fori_loop(0, rows, flatten, 0, unroll=4)
    lane = lane_ids((8, LANES))

    def load_point(group):
        return [ptf[pl.ds(group * 64 + at, 8, stride=8), :] for at in range(8)]

    def point_sums(group, unused):
        here = pl.ds(pl.multiple_of(group * 8, 8), 8)
        there = pl.ds(pl.multiple_of(rows + group * 8, 8), 8)
        pj = load_point(group)
        key = point_ref[here, :]
        entries = []
        for row_at in range(3):
            for col_at in range(row_at, 3):
                entries.append(pj[row_at] * pj[col_at] + pj[3 + row_at] * pj[3 + col_at])
        for row_at in range(3):
            entries.append(pj[row_at] * pj[6] + pj[3 + row_at] * pj[7])
        steps = [1, 2, 4, 8, 16, 32, 64]
        ahead = [(pltpu.roll(key, step, 1) == key) & (lane >= step) for step in steps]
        behind = [
            (pltpu.roll(key, LANES - step, 1) == key) & (lane < LANES - step) for step in steps
        ]
        heads = jnp.zeros((8, LANES), jnp.float32)
        tails = jnp.zeros((8, LANES), jnp.float32)
        for at, entry in enumerate(entries):
            up, down = entry, entry
            for pos, step in enumerate(steps):
                up = up + jnp.where(ahead[pos], pltpu.roll(up, step, 1), 0.0)
                down = down + jnp.where(behind[pos], pltpu.roll(down, LANES - step, 1), 0.0)
            total = up + down - entry
            xs[at, here, :] = total
            moved = total if at == 0 else pltpu.roll(total, at, 1)
            heads = jnp.where(lane == at, moved, heads)
            tails = jnp.where(lane == at, pltpu.roll(total, at + 1, 1), tails)
        first = jnp.broadcast_to(key[:, 0:1], (8, LANES))
        last = jnp.broadcast_to(key[:, LANES - 1 : LANES], (8, LANES))
        ends[here, :] = heads
        ends[there, :] = jnp.where(first != last, tails, 0.0)
        keys[here, :] = first
        keys[there, :] = last
        return unused

    lax.fori_loop(0, groups, point_sums, 0)
    match = jnp.where(keys[...] == keys[...].T, 1.0, 0.0)
    fixed[...] = jnp.dot(
        match, ends[...], precision=lax.Precision.HIGHEST, preferred_element_type=jnp.float32
    )

    def obs_terms(group, unused):
        here = pl.ds(pl.multiple_of(group * 8, 8), 8)
        there = pl.ds(pl.multiple_of(rows + group * 8, 8), 8)
        key = point_ref[here, :]
        at_first = key == keys[here, :]
        at_last = key == keys[there, :]
        head, tail = fixed[here, :], fixed[there, :]
        sums = [
            jnp.where(
                at_first, head[:, at : at + 1],
                jnp.where(at_last, tail[:, at : at + 1], xs[at, here, :]),
            )
            for at in range(9)
        ]
        v00, v01, v02 = sums[0] + DAMP, sums[1], sums[2]
        v11, v12, v22 = sums[3] + DAMP, sums[4], sums[5] + DAMP
        c00 = v11 * v22 - v12 * v12
        c01 = v02 * v12 - v01 * v22
        c02 = v01 * v12 - v02 * v11
        c11 = v00 * v22 - v02 * v02
        c12 = v01 * v02 - v00 * v12
        c22 = v00 * v11 - v01 * v01
        scale = 1.0 / (v00 * c00 + v01 * c01 + v02 * c02)
        i00, i01, i02 = c00 * scale, c01 * scale, c02 * scale
        i11, i12, i22 = c11 * scale, c12 * scale, c22 * scale
        weights = [
            i00 * sums[6] + i01 * sums[7] + i02 * sums[8],
            i01 * sums[6] + i11 * sums[7] + i12 * sums[8],
            i02 * sums[6] + i12 * sums[7] + i22 * sums[8],
        ]
        pj = load_point(group)
        vinv = ((i00, i01, i02), (i01, i11, i12), (i02, i12, i22))
        prow = [pj[0:3], pj[3:6]]
        usage = [
            [sum(vinv[outer][at] * prow[rowp][at] for at in range(3)) for outer in range(3)]
            for rowp in range(2)
        ]
        zz = sum(prow[0][at] * usage[0][at] for at in range(3))
        zo = sum(prow[0][at] * usage[1][at] for at in range(3))
        oo = sum(prow[1][at] * usage[1][at] for at in range(3))
        keep_z, keep_m, keep_o = 1.0 - zz, -zo, 1.0 - oo
        shifted = [
            pj[6 + rowp] - sum(prow[rowp][at] * weights[at] for at in range(3)) for rowp in range(2)
        ]
        cj = [camf[pl.ds(group * 192 + at, 8, stride=24), :] for at in range(18)]
        for at in range(9):
            red_ref[at, here, :] = cj[at] * shifted[0] + cj[9 + at] * shifted[1]
        for col_at in range(9):
            mixed_z = keep_z * cj[col_at] + keep_m * cj[9 + col_at]
            mixed_o = keep_m * cj[col_at] + keep_o * cj[9 + col_at]
            for row_at in range(col_at, 9):
                pos = POSITION[row_at, col_at]
                terms[pl.ds(group * 8 * WIDTH + pos, 8, stride=WIDTH), :] = (
                    cj[row_at] * mixed_z + cj[9 + row_at] * mixed_o
                )
        blank = jnp.zeros((8, LANES), jnp.float32)
        for pos in range(len(PAIRS), WIDTH):
            terms[pl.ds(group * 8 * WIDTH + pos, 8, stride=WIDTH), :] = blank
        return unused

    lax.fori_loop(0, groups, obs_terms, 0)
    camera_of_slots(slot_ref, cof)

    def widen(tile, unused):
        lanes = pl.ds(pl.multiple_of(tile * LANES, LANES), LANES)
        high, low = split_rows(terms[pl.ds(pl.multiple_of(tile * WIDTH, 8), WIDTH), :])
        blank = jnp.zeros((HALF - WIDTH, LANES), jnp.bfloat16)
        wide[0:WIDTH, lanes] = high
        wide[WIDTH:HALF, lanes] = blank
        wide[HALF : HALF + WIDTH, lanes] = low
        wide[HALF + WIDTH : LANES, lanes] = blank
        return unused

    lax.fori_loop(0, rows, widen, 0, unroll=2)
    acc[...] = jnp.zeros_like(acc)
    tiles = CHUNK // LANES

    def add_cameras(chunk, unused):
        onehot = onehot_chunk(cof, camera_ref, chunk * tiles, tiles)
        lanes = pl.ds(pl.multiple_of(chunk * CHUNK, CHUNK), CHUNK)
        acc[...] += lax.dot_general(
            onehot, wide[:, lanes], (((1,), (1,)), ((), ())), preferred_element_type=jnp.float32
        )
        return unused

    lax.fori_loop(0, rows // tiles, add_cameras, 0)

    def pack(owner, unused):
        base = pl.multiple_of(owner * 16, 16)
        top = acc[pl.ds(base, 8), :]
        low = acc[pl.ds(base + 8, 8), :]
        top = top + pltpu.roll(top, HALF, 1)
        low = low + pltpu.roll(low, HALF, 1)
        part_ref[owner, :, :] = jnp.where(lane < HALF, top, low)
        return unused

    lax.fori_loop(0, part_ref.shape[0], pack, 0, unroll=4)


def chol_inverse(entry):
    inv_root, factor = {}, {}
    for col_at in range(9):
        diag = entry[col_at, col_at] + DAMP
        for inner in range(col_at):
            diag = diag - factor[col_at, inner] * factor[col_at, inner]
        inv_root[col_at] = 1.0 / jnp.sqrt(diag)
        for row_at in range(col_at + 1, 9):
            value = entry[row_at, col_at]
            for inner in range(col_at):
                value = value - factor[row_at, inner] * factor[col_at, inner]
            factor[row_at, col_at] = value * inv_root[col_at]
    solved = {}
    for col_at in range(9):
        solved[col_at, col_at] = inv_root[col_at]
        for row_at in range(col_at + 1, 9):
            value = factor[row_at, col_at] * solved[col_at, col_at]
            for inner in range(col_at + 1, row_at):
                value = value + factor[row_at, inner] * solved[inner, col_at]
            solved[row_at, col_at] = -value * inv_root[row_at]
    result = {}
    for row_at, col_at in PAIRS:
        value = solved[row_at, row_at] * solved[row_at, col_at]
        for inner in range(row_at + 1, 9):
            value = value + solved[inner, row_at] * solved[inner, col_at]
        result[row_at, col_at] = value
    return result


def exchange_kernel(
    devices, grps, part_ref, inv_ref, table_ref, recv, square, back, gath, msg,
    send_a, recv_a, send_b, recv_b,
):
    me = lax.axis_index("pts") * grps + lax.axis_index("grp")

    def coords(peer):
        return (peer // grps, lax.rem(peer, grps))

    def peer_at(step):
        return lax.rem(me + step, devices)

    barrier = pltpu.get_barrier_semaphore()

    def greet(step, unused):
        pl.semaphore_signal(
            barrier, inc=1, device_id=coords(peer_at(step)), device_id_type=pl.DeviceIdType.MESH
        )
        return unused

    lax.fori_loop(1, devices, greet, 0)
    pl.semaphore_wait(barrier, devices - 1)

    def scatter(step):
        peer = peer_at(step)
        return pltpu.make_async_remote_copy(
            src_ref=part_ref.at[peer], dst_ref=recv.at[step],
            send_sem=send_a.at[step], recv_sem=recv_a.at[step],
            device_id=coords(peer), device_id_type=pl.DeviceIdType.MESH,
        )

    def start_scatter(step, unused):
        scatter(step).start()
        return unused

    def end_scatter(step, total):
        scatter(step).wait_recv()
        return total + recv[step]

    lax.fori_loop(1, devices, start_scatter, 0)
    total = lax.fori_loop(1, devices, end_scatter, part_ref[me])
    lane = lane_ids((8, LANES))
    square[...] = jnp.zeros_like(square)
    square[0:8, :] = total
    square[8:16, :] = pltpu.roll(total, HALF, 1)
    back[...] = square[...].T
    entry = {pair: back[pos : pos + 1, :] for pair, pos in POSITION.items()}
    result = chol_inverse(entry)
    square[...] = jnp.zeros_like(square)
    own = inv_ref.shape[1]
    for (row_at, col_at), pos in POSITION.items():
        value = result[row_at, col_at]
        square[pos : pos + 1, :] = value
        inv_ref[row_at * 9 + col_at : row_at * 9 + col_at + 1, :] = value[:, :own]
        if row_at != col_at:
            inv_ref[col_at * 9 + row_at : col_at * 9 + row_at + 1, :] = value[:, :own]
    back[...] = square[...].T
    msg[...] = jnp.where(lane < HALF, back[0:8, :], pltpu.roll(back[8:16, :], HALF, 1))

    def gather(step):
        return pltpu.make_async_remote_copy(
            src_ref=msg, dst_ref=gath.at[me],
            send_sem=send_b.at[step], recv_sem=recv_b.at[step],
            device_id=coords(peer_at(step)), device_id_type=pl.DeviceIdType.MESH,
        )

    def start_gather(step, unused):
        gather(step).start()
        return unused

    lax.fori_loop(1, devices, start_gather, 0)
    table_ref[me] = msg[...]

    def end_gather(step, unused):
        source = lax.rem(me - step + devices, devices)
        pltpu.make_async_remote_copy(
            src_ref=msg, dst_ref=gath.at[source],
            send_sem=send_b.at[step], recv_sem=recv_b.at[step],
            device_id=coords(peer_at(step)), device_id_type=pl.DeviceIdType.MESH,
        ).wait_recv()
        table_ref[source] = gath[source]
        return unused

    lax.fori_loop(1, devices, end_gather, 0)

    def drain(step, unused):
        scatter(step).wait_send()
        gather(step).wait_send()
        return unused

    lax.fori_loop(1, devices, drain, 0)


def apply_kernel(
    table_ref, inv_in_ref, red_ref, camera_ref, slot_ref, inv_ref, out_ref,
    tall, wide, cof, picked, flat,
):
    rows = camera_ref.shape[0]
    groups = rows // 8
    slots = cof.shape[0]
    inv_ref[...] = inv_in_ref[...]
    camera_of_slots(slot_ref, cof)

    def unpack(owner, unused):
        value = table_ref[owner]
        base = pl.multiple_of(owner * 16, 16)
        tall[pl.ds(base, 8), :] = value
        tall[pl.ds(base + 8, 8), :] = pltpu.roll(value, HALF, 1)
        return unused

    lax.fori_loop(0, table_ref.shape[0], unpack, 0, unroll=4)
    for block in range(slots // LANES):
        at = slice(block * LANES, (block + 1) * LANES)
        high, low = split_rows(tall[at, :].T[0:HALF, :])
        wide[0:HALF, at] = high
        wide[HALF:LANES, at] = low
    tiles = CHUNK // LANES

    def pick(chunk, unused):
        onehot = onehot_chunk(cof, camera_ref, chunk * tiles, tiles)
        both = jnp.dot(wide[...], onehot, preferred_element_type=jnp.float32)
        value = both[0:WIDTH, :] + both[HALF : HALF + WIDTH, :]
        for inner in range(tiles):
            base = pl.multiple_of((chunk * tiles + inner) * WIDTH, 8)
            picked[pl.ds(base, WIDTH), :] = value[:, inner * LANES : (inner + 1) * LANES]
        return unused

    lax.fori_loop(0, rows // tiles, pick, 0)

    def apply(group, unused):
        here = pl.ds(pl.multiple_of(group * 8, 8), 8)
        reduced = [red_ref[at, here, :] for at in range(9)]
        totals = [None] * 9
        for (row_at, col_at), pos in POSITION.items():
            value = picked[pl.ds(group * 8 * WIDTH + pos, 8, stride=WIDTH), :]
            for left, right in sorted({(row_at, col_at), (col_at, row_at)}):
                add = value * reduced[right]
                totals[left] = add if totals[left] is None else totals[left] + add
        for at in range(9):
            flat[pl.ds(group * 128 + at, 8, stride=16), :] = totals[at]
        return unused

    lax.fori_loop(0, groups, apply, 0)

    def unflatten(tile, unused):
        lanes = pl.ds(pl.multiple_of(tile * LANES, LANES), LANES)
        base = pl.multiple_of(tile * 16, 16)
        out_ref[0:8, lanes] = flat[pl.ds(base, 8), :]
        out_ref[8:9, lanes] = flat[pl.ds(base + 8, 1), :]
        return unused

    lax.fori_loop(0, rows, unflatten, 0, unroll=4)


def shards(devices, grps, cam_jac, pt_jac, resid, obs_point, obs_camera, camera_slot):
    count = obs_point.shape[0]
    slots = camera_slot.shape[0]
    own = slots // devices
    assert own == 16 and count % GROUP == 0 and slots % LANES == 0
    rows = count // LANES
    points = obs_point.reshape(rows, LANES)
    cameras = obs_camera.reshape(rows, LANES)
    slot_rows = camera_slot.reshape(slots // LANES, LANES)
    f32, bf16 = jnp.float32, jnp.bfloat16
    vmem = pl.BlockSpec(memory_space=pltpu.VMEM)
    params = functools.partial(pltpu.CompilerParams, vmem_limit_bytes=VMEM_LIMIT)
    part, reduced = pl.pallas_call(
        local_kernel,
        name="local",
        out_shape=(
            jax.ShapeDtypeStruct((devices, 8, LANES), f32),
            jax.ShapeDtypeStruct((9, rows, LANES), f32),
        ),
        in_specs=[vmem] * 6,
        out_specs=(vmem, vmem),
        scratch_shapes=[
            pltpu.VMEM((rows * 24, LANES), f32),
            pltpu.VMEM((rows * 8, LANES), f32),
            pltpu.VMEM((9, rows, LANES), f32),
            pltpu.VMEM((2 * rows, LANES), f32),
            pltpu.VMEM((2 * rows, LANES), jnp.int32),
            pltpu.VMEM((2 * rows, LANES), f32),
            pltpu.VMEM((rows * WIDTH, LANES), f32),
            pltpu.VMEM((LANES, count), bf16),
            pltpu.VMEM((slots, LANES), jnp.int32),
            pltpu.VMEM((slots, LANES), f32),
        ],
        compiler_params=params(),
    )(cam_jac, pt_jac, resid, points, cameras, slot_rows)
    dma = pltpu.SemaphoreType.DMA((devices,))
    inverse, table = pl.pallas_call(
        functools.partial(exchange_kernel, devices, grps),
        name="exchange",
        out_shape=(
            jax.ShapeDtypeStruct((81, own), f32),
            jax.ShapeDtypeStruct((devices, 8, LANES), f32),
        ),
        in_specs=[vmem],
        out_specs=(vmem, vmem),
        scratch_shapes=[
            pltpu.VMEM((devices, 8, LANES), f32),
            pltpu.VMEM((LANES, LANES), f32),
            pltpu.VMEM((LANES, LANES), f32),
            pltpu.VMEM((devices, 8, LANES), f32),
            pltpu.VMEM((8, LANES), f32),
            dma, dma, dma, dma,
        ],
        compiler_params=params(collective_id=0, has_side_effects=True),
    )(part)
    return pl.pallas_call(
        apply_kernel,
        name="apply",
        out_shape=(
            jax.ShapeDtypeStruct((81, own), f32),
            jax.ShapeDtypeStruct((9, count), f32),
        ),
        in_specs=[vmem] * 5,
        out_specs=(vmem, vmem),
        scratch_shapes=[
            pltpu.VMEM((slots, LANES), f32),
            pltpu.VMEM((LANES, slots), bf16),
            pltpu.VMEM((slots, LANES), jnp.int32),
            pltpu.VMEM((rows * WIDTH, LANES), f32),
            pltpu.VMEM((rows * 16, LANES), f32),
        ],
        compiler_params=params(),
    )(table, inverse, reduced, cameras, slot_rows)


def solution(mesh):
    grps = mesh.shape["grp"]
    devices = mesh.shape["pts"] * grps
    both = ("pts", "grp")
    in_specs = (P(None, both), P(None, both), P(None, both), P(both), P(both), P())
    return jax.shard_map(
        functools.partial(shards, devices, grps),
        mesh=mesh,
        in_specs=in_specs,
        out_specs=(P(None, both), P(None, both)),
        check_vma=False,
    )
```

time: 432 us -> 45.1 us (0.10); the launches traced: 427 us -> 44.7 us
  waiting for transfers between devices: 138 us -> 0 us
  local copies, waits for them, and re-layouts: 81 us -> 5.78 us
  matrix products: 60.8 us -> 0 us
  loops' own time: 60.8 us -> 0 us
  Pallas kernels: 0 us -> 38.3 us
  blocking collectives: 37.2 us -> 0 us
  other arithmetic: 34.4 us -> 0 us
  between operations: 14.5 us -> 0.65 us
    unnamed x2 -> x0, waiting for transfers between devices: 138 us -> none
    another operation x4 -> x0, loops' own time: 60.8 us -> none  [the longest x1 30.4 us: point_table(): lax.scan(add_block, jnp.zeros((9, npoints + SPAN), jnp.float32), (pieces,...]
    dot_general x64 -> x0, matrix products: 60.8 us -> none  [exact_dot(): jnp.dot(left, right, precision=lax.Precision.HIGHEST, preferred_element_t...]
    dynamic_slice x64 -> x0, local copies, waits for them, and re-layouts: 43.9 us -> none  [point_table(): lax.scan(add_block, jnp.zeros((9, npoints + SPAN), jnp.float32), (pieces,...]
    pallas_call x0 -> x3, Pallas kernels: none -> 38.3 us  [the longest x1 19.4 us: shards(): pl.pallas_call(functools.partial(exchange_kernel, devices, grps), name='e...]
    all_gather x1 -> x0, blocking collectives: 37.2 us -> none  [shards(): table = lax.all_gather(outgoing, ('pts', 'grp'), axis=1, tiled=True)]
    sub x34 -> x0, other arithmetic: 21.1 us -> none  [the longest x16 10.1 us: pick_block(): points[:, None] - first == window_ids[None, :]]
    add x32 -> x0, other arithmetic: 12.7 us -> none  [the longest x9 5.5 us: obs_terms(): cam_jac[row_at] * mixed[0][col_at] + cam_jac[9 + row_at] * mixed[1][col_at]]
  transfers between devices with their start and end apart: 1 -> 0, of which waited for: 1 -> 0; matrix products, arithmetic and copies ran while one was open for 0% -> 0% of each run, Pallas kernels for 0% -> 0%
where the time goes in v1:
time: 45.1 us; the launch traced here: 44.7 us
  Pallas kernels  38.3 us (85%)
  local copies, waits for them, and re-layouts  5.78 us (13%)
  between operations  0.65 us (1%)
    pallas_call x1, Pallas kernels, shards(): pl.pallas_call(functools.partial(exchange_kernel, devices, grps), name='e...  19.4 us
    pallas_call x1, Pallas kernels, shards(): pl.pallas_call(local_kernel, name='local', out_shape=(jax.ShapeDtypeStruc...  12.7 us
    pallas_call x1, Pallas kernels, shards(): pl.pallas_call(apply_kernel, name='apply', out_shape=(jax.ShapeDtypeStruc...  6.15 us
    unnamed x12, local copies, waits for them, and re-layouts  5.11 us

profile of v1, /device:TPU:0, one launch (start us, length us, event | category | flops | bytes accessed | tf_op | source)
XLA Modules:
  0.0 44.7 jit_solution(1703831754493497510)
XLA Ops:
  0.6 0.0 copy-start.5
  0.6 0.7 %copy-done.5 = s32[512]{0:T(512)S(1)} copy-done((s32[512]{0:T(512)S(1)}, s32[512]{0:T(512)}, u32[]{:S(2)}) %copy-start.5) | copy-done | bytes 2072
  1.3 0.0 copy-start
  1.3 1.1 %copy-done = f32[18,8192]{1,0:T(8,128)S(1)} copy-done((f32[18,8192]{1,0:T(8,128)S(1)}, f32[18,8192]{1,0:T(8,128)}, u32[]{:S(2)}) %copy-start) | copy-done | bytes 589848
  2.4 0.0 copy-start.1
  2.5 0.9 %copy-done.1 = f32[6,8192]{1,0:T(8,128)S(1)} copy-done((f32[6,8192]{1,0:T(8,128)S(1)}, f32[6,8192]{1,0:T(8,128)}, u32[]{:S(2)}) %copy-start.1) | copy-done | bytes 196632
  3.4 0.0 copy-start.2
  3.4 0.8 %copy-done.2 = s32[8192]{0:T(1024)S(1)} copy-done((s32[8192]{0:T(1024)S(1)}, s32[8192]{0:T(1024)}, u32[]{:S(2)}) %copy-start.2) | copy-done | bytes 32792
  4.2 0.0 copy-start.3
  4.2 0.8 %copy-done.3 = f32[2,8192]{1,0:T(2,128)S(1)} copy-done((f32[2,8192]{1,0:T(2,128)S(1)}, f32[2,8192]{1,0:T(2,128)}, u32[]{:S(2)}) %copy-start.3) | copy-done | bytes 65560
  5.0 0.0 copy-start.4
  5.0 0.8 %copy-done.4 = s32[8192]{0:T(1024)S(1)} copy-done((s32[8192]{0:T(1024)S(1)}, s32[8192]{0:T(1024)}, u32[]{:S(2)}) %copy-start.4) | copy-done | bytes 32792
  5.8 12.7 %local.1 = (f32[32,8,128]{2,1,0:T(8,128)S(1)}, f32[9,64,128]{2,1,0:T(8,128)S(1)}) custom-call(f32[18,8192]{1,0:T(8,128)S(1)} %copy-done, f32[6,8192]{1,0:T(8,128)S(1)} %copy-done.1, f32[2,8192]{1,0:T(2,128)S(1)} %copy-done.3, s32[64,128]{1,0:T(8,128)S(1)} %bitcast.5, s32[64,128]{1,0:T(8,128)S(1)} %bitcast.3, s32[4,128]{1,0:T(4,128)S(1)} %bitcast.6), custom_call_target="tpu_custom_call" | custom-call | tf_op jit(solution)/shard_map/local/pallas_call | solution.py:416
  18.5 19.4 %exchange.1 = (f32[81,16]{1,0:T(8,128)S(1)}, f32[32,8,128]{2,1,0:T(8,128)S(1)}) custom-call(f32[32,8,128]{2,1,0:T(8,128)S(1)} %get-tuple-element.6.part_ref), custom_call_target="tpu_custom_call" | custom-call | tf_op jit(solution)/shard_map/exchange/pallas_call | solution.py:440
  37.9 6.2 %apply.1 = (f32[81,16]{1,0:T(8,128)S(1)}, f32[9,8192]{1,0:T(8,128)}) custom-call(f32[32,8,128]{2,1,0:T(8,128)S(1)} %get-tuple-element.7.table_ref, f32[81,16]{1,0:T(8,128)S(1)} %get-tuple-element.8.inv_in_ref, f32[9,64,128]{2,1,0:T(8,128)S(1)} %get-tuple-element.9.red_ref, s32[64,128]{1,0:T(8,128)S(1)} %bitcast.4, s32[4,128]{1,0:T(4,128)S(1)} %bitcast.7), custom_call_target="tpu_custom_call" | custom-call | tf_op jit(solution)/shard_map/apply/pallas_call | solution.py:459
  44.0 0.7 %copy.8 = f32[81,16]{0,1:T(8,128)} copy(f32[81,16]{1,0:T(8,128)S(1)} %get-tuple-element.10) | data formatting | bytes 10368 | tf_op jit(solution)/shard_map/apply/pallas_call | solution.py:459
Async XLA Ops:
  0.6 0.7 %copy-start.5 = (s32[512]{0:T(512)S(1)}, s32[512]{0:T(512)}, u32[]{:S(2)}) copy-start(s32[512]{0:T(512)} %param.11) | copy-start | bytes 6148
  1.3 1.1 %copy-start = (f32[18,8192]{1,0:T(8,128)S(1)}, f32[18,8192]{1,0:T(8,128)}, u32[]{:S(2)}) copy-start(f32[18,8192]{1,0:T(8,128)} %cam_ref.1) | copy-start | bytes 1769476
  2.4 0.9 %copy-start.1 = (f32[6,8192]{1,0:T(8,128)S(1)}, f32[6,8192]{1,0:T(8,128)}, u32[]{:S(2)}) copy-start(f32[6,8192]{1,0:T(8,128)} %pt_ref.1) | copy-start | bytes 589828
  3.4 0.8 %copy-start.2 = (s32[8192]{0:T(1024)S(1)}, s32[8192]{0:T(1024)}, u32[]{:S(2)}) copy-start(s32[8192]{0:T(1024)} %param.10) | copy-start | bytes 98308
  4.2 0.8 %copy-start.3 = (f32[2,8192]{1,0:T(2,128)S(1)}, f32[2,8192]{1,0:T(2,128)}, u32[]{:S(2)}) copy-start(f32[2,8192]{1,0:T(2,128)} %res_ref.1) | copy-start | bytes 196612
  5.0 0.8 %copy-start.4 = (s32[8192]{0:T(1024)S(1)}, s32[8192]{0:T(1024)}, u32[]{:S(2)}) copy-start(s32[8192]{0:T(1024)} %param.9) | copy-start | bytes 98308

commit v2 on v1

--- a/solution.py
+++ b/solution.py
@@ -15,7 +15,7 @@
 CHUNK = 512
 PAIRS = [(row_at, col_at) for row_at in range(9) for col_at in range(row_at + 1)]
 POSITION = {pair: pos for pos, pair in enumerate(PAIRS)}
-VMEM_LIMIT = 48 * 1024 * 1024
+VMEM_LIMIT = 40 * 1024 * 1024
 
 
 def lane_ids(shape):
@@ -35,17 +35,24 @@
             hit = slot_ref[part : part + 1, :] == ids
             total = total + jnp.where(hit, named.astype(jnp.float32), 0.0)
         camera = jnp.sum(total, axis=1, keepdims=True)
-        cof_ref[pl.ds(base, block), :] = jnp.broadcast_to(camera, (block, LANES)).astype(jnp.int32)
+        wide = jnp.broadcast_to(camera, (block, LANES)).astype(jnp.int32)
+        cof_ref[pl.ds(base, block), :] = wide.astype(jnp.int16)
         return unused
 
     lax.fori_loop(0, slots // block, one, 0)
 
 
 def onehot_chunk(cof_ref, camera_ref, first, count):
+    one, zero = jnp.ones((16, LANES), jnp.bfloat16), jnp.zeros((16, LANES), jnp.bfloat16)
     pieces = []
     for inner in range(count):
-        named = camera_ref[pl.ds(first + inner, 1), :]
-        pieces.append(jnp.where(cof_ref[...] == named, 1.0, 0.0).astype(jnp.bfloat16))
+        named = jnp.broadcast_to(camera_ref[pl.ds(first + inner, 1), :], (16, LANES))
+        named = named.astype(jnp.int16)
+        blocks = [
+            jnp.where(cof_ref[at : at + 16, :] == named, one, zero)
+            for at in range(0, cof_ref.shape[0], 16)
+        ]
+        pieces.append(jnp.concatenate(blocks, axis=0))
     return jnp.concatenate(pieces, axis=1)
 
 
@@ -54,11 +61,75 @@
     return high, (value - high.astype(jnp.float32)).astype(jnp.bfloat16)
 
 
-def local_kernel(
-    cam_ref, pt_ref, res_ref, point_ref, camera_ref, slot_ref,
-    part_ref, red_ref,
-    camf, ptf, xs, ends, keys, fixed, terms, wide, cof, acc,
+def chol_inverse(entry):
+    inv_root, factor = {}, {}
+    for col_at in range(9):
+        diag = entry[col_at, col_at] + DAMP
+        for inner in range(col_at):
+            diag = diag - factor[col_at, inner] * factor[col_at, inner]
+        inv_root[col_at] = 1.0 / jnp.sqrt(diag)
+        for row_at in range(col_at + 1, 9):
+            value = entry[row_at, col_at]
+            for inner in range(col_at):
+                value = value - factor[row_at, inner] * factor[col_at, inner]
+            factor[row_at, col_at] = value * inv_root[col_at]
+    solved = {}
+    for col_at in range(9):
+        solved[col_at, col_at] = inv_root[col_at]
+        for row_at in range(col_at + 1, 9):
+            value = factor[row_at, col_at] * solved[col_at, col_at]
+            for inner in range(col_at + 1, row_at):
+                value = value + factor[row_at, inner] * solved[inner, col_at]
+            solved[row_at, col_at] = -value * inv_root[row_at]
+    result = {}
+    for row_at, col_at in PAIRS:
+        value = solved[row_at, row_at] * solved[row_at, col_at]
+        for inner in range(row_at + 1, 9):
+            value = value + solved[inner, row_at] * solved[inner, col_at]
+        result[row_at, col_at] = value
+    return result
+
+
+def sums_kernel(
+    devices, grps,
+    cam_hbm, pt_hbm, res_hbm, point_hbm, camera_hbm, slot_hbm,
+    red_ref, inv_ref, table_ref, cof, camera_ref,
+    cam_ref, pt_ref, res_ref, point_ref, slot_ref, part_ref,
+    camf, ptf, xs, ends, keys, fixed, terms, wide, acc,
+    recv, square, back, gath, msg, load_sem, send_a, recv_a, send_b, recv_b,
 ):
+    loads = [
+        pltpu.make_async_copy(source, target, load_sem.at[at])
+        for at, (source, target) in enumerate(
+            [
+                (slot_hbm, slot_ref), (pt_hbm, pt_ref), (res_hbm, res_ref),
+                (point_hbm, point_ref), (cam_hbm, cam_ref), (camera_hbm, camera_ref),
+            ]
+        )
+    ]
+    for load in loads:
+        load.start()
+    me = lax.axis_index("pts") * grps + lax.axis_index("grp")
+
+    def coords(peer):
+        return (peer // grps, lax.rem(peer, grps))
+
+    def peer_at(step):
+        return lax.rem(me + step, devices)
+
+    barrier = pltpu.get_barrier_semaphore()
+
+    def greet(step, unused):
+        pl.semaphore_signal(
+            barrier, inc=1, device_id=coords(peer_at(step)), device_id_type=pl.DeviceIdType.MESH
+        )
+        return unused
+
+    lax.fori_loop(1, devices, greet, 0)
+    loads[0].wait()
+    camera_of_slots(slot_ref, cof)
+    for load in loads[1:]:
+        load.wait()
     rows = point_ref.shape[0]
     groups = rows // 8
 
@@ -180,7 +251,6 @@
         return unused
 
     lax.fori_loop(0, groups, obs_terms, 0)
-    camera_of_slots(slot_ref, cof)
 
     def widen(tile, unused):
         lanes = pl.ds(pl.multiple_of(tile * LANES, LANES), LANES)
@@ -216,58 +286,6 @@
         return unused
 
     lax.fori_loop(0, part_ref.shape[0], pack, 0, unroll=4)
-
-
-def chol_inverse(entry):
-    inv_root, factor = {}, {}
-    for col_at in range(9):
-        diag = entry[col_at, col_at] + DAMP
-        for inner in range(col_at):
-            diag = diag - factor[col_at, inner] * factor[col_at, inner]
-        inv_root[col_at] = 1.0 / jnp.sqrt(diag)
-        for row_at in range(col_at + 1, 9):
-            value = entry[row_at, col_at]
-            for inner in range(col_at):
-                value = value - factor[row_at, inner] * factor[col_at, inner]
-            factor[row_at, col_at] = value * inv_root[col_at]
-    solved = {}
-    for col_at in range(9):
-        solved[col_at, col_at] = inv_root[col_at]
-        for row_at in range(col_at + 1, 9):
-            value = factor[row_at, col_at] * solved[col_at, col_at]
-            for inner in range(col_at + 1, row_at):
-                value = value + factor[row_at, inner] * solved[inner, col_at]
-            solved[row_at, col_at] = -value * inv_root[row_at]
-    result = {}
-    for row_at, col_at in PAIRS:
-        value = solved[row_at, row_at] * solved[row_at, col_at]
-        for inner in range(row_at + 1, 9):
-            value = value + solved[inner, row_at] * solved[inner, col_at]
-        result[row_at, col_at] = value
-    return result
-
-
-def exchange_kernel(
-    devices, grps, part_ref, inv_ref, table_ref, recv, square, back, gath, msg,
-    send_a, recv_a, send_b, recv_b,
-):
-    me = lax.axis_index("pts") * grps + lax.axis_index("grp")
-
-    def coords(peer):
-        return (peer // grps, lax.rem(peer, grps))
-
-    def peer_at(step):
-        return lax.rem(me + step, devices)
-
-    barrier = pltpu.get_barrier_semaphore()
-
-    def greet(step, unused):
-        pl.semaphore_signal(
-            barrier, inc=1, device_id=coords(peer_at(step)), device_id_type=pl.DeviceIdType.MESH
-        )
-        return unused
-
-    lax.fori_loop(1, devices, greet, 0)
     pl.semaphore_wait(barrier, devices - 1)
 
     def scatter(step):
@@ -288,7 +306,6 @@
 
     lax.fori_loop(1, devices, start_scatter, 0)
     total = lax.fori_loop(1, devices, end_scatter, part_ref[me])
-    lane = lane_ids((8, LANES))
     square[...] = jnp.zeros_like(square)
     square[0:8, :] = total
     square[8:16, :] = pltpu.roll(total, HALF, 1)
@@ -341,14 +358,14 @@
 
 
 def apply_kernel(
-    table_ref, inv_in_ref, red_ref, camera_ref, slot_ref, inv_ref, out_ref,
-    tall, wide, cof, picked, flat,
+    table_ref, inv_in_ref, red_ref, cof, camera_ref, inv_ref, out_ref,
+    tall, wide, picked, flat, out, inv_sem, out_sem,
 ):
     rows = camera_ref.shape[0]
     groups = rows // 8
     slots = cof.shape[0]
-    inv_ref[...] = inv_in_ref[...]
-    camera_of_slots(slot_ref, cof)
+    inv_copy = pltpu.make_async_copy(inv_in_ref, inv_ref, inv_sem)
+    inv_copy.start()
 
     def unpack(owner, unused):
         value = table_ref[owner]
@@ -365,40 +382,43 @@
         wide[HALF:LANES, at] = low
     tiles = CHUNK // LANES
 
-    def pick(chunk, unused):
-        onehot = onehot_chunk(cof, camera_ref, chunk * tiles, tiles)
-        both = jnp.dot(wide[...], onehot, preferred_element_type=jnp.float32)
-        value = both[0:WIDTH, :] + both[HALF : HALF + WIDTH, :]
-        for inner in range(tiles):
-            base = pl.multiple_of((chunk * tiles + inner) * WIDTH, 8)
-            picked[pl.ds(base, WIDTH), :] = value[:, inner * LANES : (inner + 1) * LANES]
-        return unused
-
-    lax.fori_loop(0, rows // tiles, pick, 0)
+    def out_copy(group):
+        lanes = pl.ds(pl.multiple_of(group * GROUP, GROUP), GROUP)
+        return pltpu.make_async_copy(out.at[:, lanes], out_ref.at[:, lanes], out_sem.at[group])
 
     def apply(group, unused):
         here = pl.ds(pl.multiple_of(group * 8, 8), 8)
+        for part in range(8 // tiles):
+            onehot = onehot_chunk(cof, camera_ref, group * 8 + part * tiles, tiles)
+            both = jnp.dot(wide[...], onehot, preferred_element_type=jnp.float32)
+            value = both[0:WIDTH, :] + both[HALF : HALF + WIDTH, :]
+            for inner in range(tiles):
+                base = (part * tiles + inner) * WIDTH
+                picked[base : base + WIDTH, :] = value[:, inner * LANES : (inner + 1) * LANES]
         reduced = [red_ref[at, here, :] for at in range(9)]
         totals = [None] * 9
         for (row_at, col_at), pos in POSITION.items():
-            value = picked[pl.ds(group * 8 * WIDTH + pos, 8, stride=WIDTH), :]
+            value = picked[pl.ds(pos, 8, stride=WIDTH), :]
             for left, right in sorted({(row_at, col_at), (col_at, row_at)}):
                 add = value * reduced[right]
                 totals[left] = add if totals[left] is None else totals[left] + add
         for at in range(9):
-            flat[pl.ds(group * 128 + at, 8, stride=16), :] = totals[at]
+            flat[pl.ds(at, 8, stride=16), :] = totals[at]
+        for inner in range(8):
+            lanes = pl.ds(pl.multiple_of(group * GROUP + inner * LANES, LANES), LANES)
+            out[0:8, lanes] = flat[inner * 16 : inner * 16 + 8, :]
+            out[8:9, lanes] = flat[inner * 16 + 8 : inner * 16 + 9, :]
+        out_copy(group).start()
         return unused
 
     lax.fori_loop(0, groups, apply, 0)
 
-    def unflatten(tile, unused):
-        lanes = pl.ds(pl.multiple_of(tile * LANES, LANES), LANES)
-        base = pl.multiple_of(tile * 16, 16)
-        out_ref[0:8, lanes] = flat[pl.ds(base, 8), :]
-        out_ref[8:9, lanes] = flat[pl.ds(base + 8, 1), :]
-        return unused
-
-    lax.fori_loop(0, rows, unflatten, 0, unroll=4)
+    def finish(group, unused):
+        out_copy(group).wait()
+        return unused
+
+    lax.fori_loop(0, groups, finish, 0)
+    inv_copy.wait()
 
 
 def shards(devices, grps, cam_jac, pt_jac, resid, obs_point, obs_camera, camera_slot):
@@ -413,16 +433,29 @@
     f32, bf16 = jnp.float32, jnp.bfloat16
     vmem = pl.BlockSpec(memory_space=pltpu.VMEM)
     params = functools.partial(pltpu.CompilerParams, vmem_limit_bytes=VMEM_LIMIT)
-    part, reduced = pl.pallas_call(
-        local_kernel,
-        name="local",
+    hbm = pl.BlockSpec(memory_space=pltpu.HBM)
+    dma = pltpu.SemaphoreType.DMA
+    square = pltpu.VMEM((LANES, LANES), f32)
+    mail = pltpu.VMEM((devices, 8, LANES), f32)
+    reduced, inverse, table, cof, named = pl.pallas_call(
+        functools.partial(sums_kernel, devices, grps),
+        name="sums",
         out_shape=(
+            jax.ShapeDtypeStruct((9, rows, LANES), f32),
+            jax.ShapeDtypeStruct((81, own), f32),
             jax.ShapeDtypeStruct((devices, 8, LANES), f32),
-            jax.ShapeDtypeStruct((9, rows, LANES), f32),
+            jax.ShapeDtypeStruct((slots, LANES), jnp.int16),
+            jax.ShapeDtypeStruct((rows, LANES), jnp.int32),
         ),
-        in_specs=[vmem] * 6,
-        out_specs=(vmem, vmem),
+        in_specs=[hbm] * 6,
+        out_specs=(vmem,) * 5,
         scratch_shapes=[
+            pltpu.VMEM((18, count), f32),
+            pltpu.VMEM((6, count), f32),
+            pltpu.VMEM((2, count), f32),
+            pltpu.VMEM((rows, LANES), jnp.int32),
+            pltpu.VMEM((slots // LANES, LANES), jnp.int32),
+            mail,
             pltpu.VMEM((rows * 24, LANES), f32),
             pltpu.VMEM((rows * 8, LANES), f32),
             pltpu.VMEM((9, rows, LANES), f32),
@@ -431,31 +464,13 @@
             pltpu.VMEM((2 * rows, LANES), f32),
             pltpu.VMEM((rows * WIDTH, LANES), f32),
             pltpu.VMEM((LANES, count), bf16),
-            pltpu.VMEM((slots, LANES), jnp.int32),
             pltpu.VMEM((slots, LANES), f32),
-        ],
-        compiler_params=params(),
-    )(cam_jac, pt_jac, resid, points, cameras, slot_rows)
-    dma = pltpu.SemaphoreType.DMA((devices,))
-    inverse, table = pl.pallas_call(
-        functools.partial(exchange_kernel, devices, grps),
-        name="exchange",
-        out_shape=(
-            jax.ShapeDtypeStruct((81, own), f32),
-            jax.ShapeDtypeStruct((devices, 8, LANES), f32),
-        ),
-        in_specs=[vmem],
-        out_specs=(vmem, vmem),
-        scratch_shapes=[
-            pltpu.VMEM((devices, 8, LANES), f32),
-            pltpu.VMEM((LANES, LANES), f32),
-            pltpu.VMEM((LANES, LANES), f32),
-            pltpu.VMEM((devices, 8, LANES), f32),
+            mail, square, square, mail,
             pltpu.VMEM((8, LANES), f32),
-            dma, dma, dma, dma,
+            dma((6,)), dma((devices,)), dma((devices,)), dma((devices,)), dma((devices,)),
         ],
         compiler_params=params(collective_id=0, has_side_effects=True),
-    )(part)
+    )(cam_jac, pt_jac, resid, points, cameras, slot_rows)
     return pl.pallas_call(
         apply_kernel,
         name="apply",
@@ -464,16 +479,18 @@
             jax.ShapeDtypeStruct((9, count), f32),
         ),
         in_specs=[vmem] * 5,
-        out_specs=(vmem, vmem),
+        out_specs=(hbm, hbm),
         scratch_shapes=[
             pltpu.VMEM((slots, LANES), f32),
             pltpu.VMEM((LANES, slots), bf16),
-            pltpu.VMEM((slots, LANES), jnp.int32),
-            pltpu.VMEM((rows * WIDTH, LANES), f32),
-            pltpu.VMEM((rows * 16, LANES), f32),
+            pltpu.VMEM((8 * WIDTH, LANES), f32),
+            pltpu.VMEM((LANES, LANES), f32),
+            pltpu.VMEM((9, count), f32),
+            dma(()),
+            dma((rows // 8,)),
         ],
         compiler_params=params(),
-    )(table, inverse, reduced, cameras, slot_rows)
+    )(table, inverse, reduced, cof, named)
 
 
 def solution(mesh):

time: 45.1 us -> 40.3 us (0.89)
  Pallas kernels: 38.3 us -> 33.4 us
    pallas_call x2 -> x1, Pallas kernels: 32.1 us -> 28.7 us  [shards(): pl.pallas_call(functools.partial(sums_kernel, devices, grps), name='sums'...]
    pallas_call x1, Pallas kernels: 6.15 us -> 4.75 us  [shards(): pl.pallas_call(apply_kernel, name='apply', out_shape=(jax.ShapeDtypeStruc...]
where the time goes in v2:
time: 40.3 us; the launch traced here: 39.9 us
  Pallas kernels  33.4 us (83%)
  local copies, waits for them, and re-layouts  5.78 us (14%)
  between operations  0.66 us (2%)
    pallas_call x1, Pallas kernels, shards(): pl.pallas_call(functools.partial(sums_kernel, devices, grps), name='sums'...  28.7 us
    unnamed x12, local copies, waits for them, and re-layouts  5.11 us
    pallas_call x1, Pallas kernels, shards(): pl.pallas_call(apply_kernel, name='apply', out_shape=(jax.ShapeDtypeStruc...  4.75 us

profile of v2, /device:TPU:0, one launch (start us, length us, event | category | flops | bytes accessed | tf_op | source)
XLA Modules:
  0.0 39.9 jit_solution(14340558705787672355)
XLA Ops:
  0.6 0.0 copy-start.5
  0.6 0.7 %copy-done.5 = s32[512]{0:T(512)S(1)} copy-done((s32[512]{0:T(512)S(1)}, s32[512]{0:T(512)}, u32[]{:S(2)}) %copy-start.5) | copy-done | bytes 2072
  1.3 0.0 copy-start
  1.3 1.1 %copy-done = f32[18,8192]{1,0:T(8,128)S(1)} copy-done((f32[18,8192]{1,0:T(8,128)S(1)}, f32[18,8192]{1,0:T(8,128)}, u32[]{:S(2)}) %copy-start) | copy-done | bytes 589848
  2.4 0.0 copy-start.1
  2.5 0.9 %copy-done.1 = f32[6,8192]{1,0:T(8,128)S(1)} copy-done((f32[6,8192]{1,0:T(8,128)S(1)}, f32[6,8192]{1,0:T(8,128)}, u32[]{:S(2)}) %copy-start.1) | copy-done | bytes 196632
  3.4 0.0 copy-start.2
  3.4 0.8 %copy-done.2 = f32[2,8192]{1,0:T(2,128)S(1)} copy-done((f32[2,8192]{1,0:T(2,128)S(1)}, f32[2,8192]{1,0:T(2,128)}, u32[]{:S(2)}) %copy-start.2) | copy-done | bytes 65560
  4.2 0.0 copy-start.3
  4.2 0.8 %copy-done.3 = s32[8192]{0:T(1024)S(1)} copy-done((s32[8192]{0:T(1024)S(1)}, s32[8192]{0:T(1024)}, u32[]{:S(2)}) %copy-start.3) | copy-done | bytes 32792
  5.0 0.0 copy-start.4
  5.0 0.8 %copy-done.4 = s32[8192]{0:T(1024)S(1)} copy-done((s32[8192]{0:T(1024)S(1)}, s32[8192]{0:T(1024)}, u32[]{:S(2)}) %copy-start.4) | copy-done | bytes 32792
  5.8 28.7 %sums.1 = (f32[9,64,128]{2,1,0:T(8,128)S(1)}, f32[81,16]{1,0:T(8,128)S(1)}, f32[32,8,128]{2,1,0:T(8,128)S(1)}, s16[512,128]{1,0:T(8,128)(2,1)S(1)}, s32[64,128]{1,0:T(8,128)S(1)}) custom-call(f32[18,8192]{1,0:T(8,128)S(1)} %copy-done, f32[6,8192]{1,0:T(8,128)S(1)} %copy-done.1, f32[2,8192]{1,0:T(2,128)S(1)} %copy-done.2, s32[64,128]{1,0:T(8,128)S(1)} %bitcast.3, ...), custom_call_target="tpu_custom_call" | custom-call | tf_op jit(solution)/shard_map/sums/pallas_call | solution.py:440
  34.4 4.7 %apply.1 = (f32[81,16]{1,0:T(8,128)S(1)}, f32[9,8192]{1,0:T(8,128)}) custom-call(f32[32,8,128]{2,1,0:T(8,128)S(1)} %get-tuple-element.7.table_ref, f32[81,16]{1,0:T(8,128)S(1)} %get-tuple-element.8.inv_in_ref, f32[9,64,128]{2,1,0:T(8,128)S(1)} %get-tuple-element.9.red_ref, s16[512,128]{1,0:T(8,128)(2,1)S(1)} %get-tuple-element.10.cof, ...), custom_call_target="tpu_custom_call" | custom-call | tf_op jit(solution)/shard_map/apply/pallas_call | solution.py:474
  39.2 0.7 %copy.8 = f32[81,16]{0,1:T(8,128)} copy(f32[81,16]{1,0:T(8,128)S(1)} %get-tuple-element.12) | data formatting | bytes 10368 | tf_op jit(solution)/shard_map/apply/pallas_call | solution.py:474
Async XLA Ops:
  0.6 0.7 %copy-start.5 = (s32[512]{0:T(512)S(1)}, s32[512]{0:T(512)}, u32[]{:S(2)}) copy-start(s32[512]{0:T(512)} %param.11) | copy-start | bytes 6148
  1.3 1.1 %copy-start = (f32[18,8192]{1,0:T(8,128)S(1)}, f32[18,8192]{1,0:T(8,128)}, u32[]{:S(2)}) copy-start(f32[18,8192]{1,0:T(8,128)} %cam_hbm.1) | copy-start | bytes 1769476
  2.4 0.9 %copy-start.1 = (f32[6,8192]{1,0:T(8,128)S(1)}, f32[6,8192]{1,0:T(8,128)}, u32[]{:S(2)}) copy-start(f32[6,8192]{1,0:T(8,128)} %pt_hbm.1) | copy-start | bytes 589828
  3.4 0.8 %copy-start.2 = (f32[2,8192]{1,0:T(2,128)S(1)}, f32[2,8192]{1,0:T(2,128)}, u32[]{:S(2)}) copy-start(f32[2,8192]{1,0:T(2,128)} %res_hbm.1) | copy-start | bytes 196612
  4.2 0.8 %copy-start.3 = (s32[8192]{0:T(1024)S(1)}, s32[8192]{0:T(1024)}, u32[]{:S(2)}) copy-start(s32[8192]{0:T(1024)} %param.9) | copy-start | bytes 98308
  5.0 0.8 %copy-start.4 = (s32[8192]{0:T(1024)S(1)}, s32[8192]{0:T(1024)}, u32[]{:S(2)}) copy-start(s32[8192]{0:T(1024)} %param.10) | copy-start | bytes 98308

commit v3 on v2

--- a/solution.py
+++ b/solution.py
@@ -15,7 +15,7 @@
 CHUNK = 512
 PAIRS = [(row_at, col_at) for row_at in range(9) for col_at in range(row_at + 1)]
 POSITION = {pair: pos for pos, pair in enumerate(PAIRS)}
-VMEM_LIMIT = 40 * 1024 * 1024
+VMEM_LIMIT = 66000000
 
 
 def lane_ids(shape):
@@ -93,10 +93,10 @@
 def sums_kernel(
     devices, grps,
     cam_hbm, pt_hbm, res_hbm, point_hbm, camera_hbm, slot_hbm,
-    red_ref, inv_ref, table_ref, cof, camera_ref,
+    red_hbm, inv_hbm, table_ref, cof_hbm, named_hbm,
     cam_ref, pt_ref, res_ref, point_ref, slot_ref, part_ref,
     camf, ptf, xs, ends, keys, fixed, terms, wide, acc,
-    recv, square, back, gath, msg, load_sem, send_a, recv_a, send_b, recv_b,
+    recv, square, back, msg, red_ref, inv_ref, cof, camera_ref, load_sem, save_sem, send_a, recv_a, send_b, recv_b,
 ):
     loads = [
         pltpu.make_async_copy(source, target, load_sem.at[at])
@@ -117,6 +117,17 @@
     def peer_at(step):
         return lax.rem(me + step, devices)
 
+    def others(body, carry):
+        for step in range(1, 8):
+            carry = body(step, carry)
+
+        def eight(block, carry):
+            for inner in range(8):
+                carry = body(block * 8 + inner, carry)
+            return carry
+
+        return lax.fori_loop(1, devices // 8, eight, carry)
+
     barrier = pltpu.get_barrier_semaphore()
 
     def greet(step, unused):
@@ -125,11 +136,20 @@
         )
         return unused
 
-    lax.fori_loop(1, devices, greet, 0)
+    others(greet, 0)
     loads[0].wait()
     camera_of_slots(slot_ref, cof)
     for load in loads[1:]:
         load.wait()
+    saves = [
+        pltpu.make_async_copy(source, target, save_sem.at[at])
+        for at, (source, target) in enumerate(
+            [(cof, cof_hbm), (camera_ref, named_hbm), (red_ref, red_hbm), (inv_ref, inv_hbm)]
+        )
+    ]
+    own_row = pltpu.make_async_copy(msg, table_ref.at[me], save_sem.at[4])
+    saves[0].start()
+    saves[1].start()
     rows = point_ref.shape[0]
     groups = rows // 8
 
@@ -251,6 +271,7 @@
         return unused
 
     lax.fori_loop(0, groups, obs_terms, 0)
+    saves[2].start()
 
     def widen(tile, unused):
         lanes = pl.ds(pl.multiple_of(tile * LANES, LANES), LANES)
@@ -304,8 +325,8 @@
         scatter(step).wait_recv()
         return total + recv[step]
 
-    lax.fori_loop(1, devices, start_scatter, 0)
-    total = lax.fori_loop(1, devices, end_scatter, part_ref[me])
+    others(start_scatter, 0)
+    total = others(end_scatter, part_ref[me])
     square[...] = jnp.zeros_like(square)
     square[0:8, :] = total
     square[8:16, :] = pltpu.roll(total, HALF, 1)
@@ -313,19 +334,15 @@
     entry = {pair: back[pos : pos + 1, :] for pair, pos in POSITION.items()}
     result = chol_inverse(entry)
     square[...] = jnp.zeros_like(square)
-    own = inv_ref.shape[1]
     for (row_at, col_at), pos in POSITION.items():
         value = result[row_at, col_at]
         square[pos : pos + 1, :] = value
-        inv_ref[row_at * 9 + col_at : row_at * 9 + col_at + 1, :] = value[:, :own]
-        if row_at != col_at:
-            inv_ref[col_at * 9 + row_at : col_at * 9 + row_at + 1, :] = value[:, :own]
     back[...] = square[...].T
     msg[...] = jnp.where(lane < HALF, back[0:8, :], pltpu.roll(back[8:16, :], HALF, 1))
 
     def gather(step):
         return pltpu.make_async_remote_copy(
-            src_ref=msg, dst_ref=gath.at[me],
+            src_ref=msg, dst_ref=table_ref.at[me],
             send_sem=send_b.at[step], recv_sem=recv_b.at[step],
             device_id=coords(peer_at(step)), device_id_type=pl.DeviceIdType.MESH,
         )
@@ -334,27 +351,35 @@
         gather(step).start()
         return unused
 
-    lax.fori_loop(1, devices, start_gather, 0)
-    table_ref[me] = msg[...]
+    others(start_gather, 0)
+    own_row.start()
+    for (row_at, col_at), value in result.items():
+        for left, right in sorted({(row_at, col_at), (col_at, row_at)}):
+            pos = left * 9 + right
+            square[pos : pos + 1, :] = value
+    inv_ref[...] = square[...].T[0 : inv_ref.shape[0], 0:81]
+    saves[3].start()
 
     def end_gather(step, unused):
         source = lax.rem(me - step + devices, devices)
         pltpu.make_async_remote_copy(
-            src_ref=msg, dst_ref=gath.at[source],
+            src_ref=msg, dst_ref=table_ref.at[source],
             send_sem=send_b.at[step], recv_sem=recv_b.at[step],
             device_id=coords(peer_at(step)), device_id_type=pl.DeviceIdType.MESH,
         ).wait_recv()
-        table_ref[source] = gath[source]
-        return unused
-
-    lax.fori_loop(1, devices, end_gather, 0)
+        return unused
+
+    others(end_gather, 0)
 
     def drain(step, unused):
         scatter(step).wait_send()
         gather(step).wait_send()
         return unused
 
-    lax.fori_loop(1, devices, drain, 0)
+    others(drain, 0)
+    for save in saves:
+        save.wait()
+    own_row.wait()
 
 
 def apply_kernel(
@@ -425,7 +450,7 @@
     count = obs_point.shape[0]
     slots = camera_slot.shape[0]
     own = slots // devices
-    assert own == 16 and count % GROUP == 0 and slots % LANES == 0
+    assert own == 16 and devices % 8 == 0 and count % GROUP == 0 and slots % LANES == 0
     rows = count // LANES
     points = obs_point.reshape(rows, LANES)
     cameras = obs_camera.reshape(rows, LANES)
@@ -442,13 +467,13 @@
         name="sums",
         out_shape=(
             jax.ShapeDtypeStruct((9, rows, LANES), f32),
-            jax.ShapeDtypeStruct((81, own), f32),
+            jax.ShapeDtypeStruct((own, 81), f32),
             jax.ShapeDtypeStruct((devices, 8, LANES), f32),
             jax.ShapeDtypeStruct((slots, LANES), jnp.int16),
             jax.ShapeDtypeStruct((rows, LANES), jnp.int32),
         ),
         in_specs=[hbm] * 6,
-        out_specs=(vmem,) * 5,
+        out_specs=(hbm,) * 5,
         scratch_shapes=[
             pltpu.VMEM((18, count), f32),
             pltpu.VMEM((6, count), f32),
@@ -465,17 +490,21 @@
             pltpu.VMEM((rows * WIDTH, LANES), f32),
             pltpu.VMEM((LANES, count), bf16),
             pltpu.VMEM((slots, LANES), f32),
-            mail, square, square, mail,
+            mail, square, square,
             pltpu.VMEM((8, LANES), f32),
-            dma((6,)), dma((devices,)), dma((devices,)), dma((devices,)), dma((devices,)),
+            pltpu.VMEM((9, rows, LANES), f32),
+            pltpu.VMEM((own, 81), f32),
+            pltpu.VMEM((slots, LANES), jnp.int16),
+            pltpu.VMEM((rows, LANES), jnp.int32),
+            dma((6,)), dma((5,)), dma((devices,)), dma((devices,)), dma((devices,)), dma((devices,)),
         ],
         compiler_params=params(collective_id=0, has_side_effects=True),
     )(cam_jac, pt_jac, resid, points, cameras, slot_rows)
-    return pl.pallas_call(
+    inverse, precond = pl.pallas_call(
         apply_kernel,
         name="apply",
         out_shape=(
-            jax.ShapeDtypeStruct((81, own), f32),
+            jax.ShapeDtypeStruct((own, 81), f32),
             jax.ShapeDtypeStruct((9, count), f32),
         ),
         in_specs=[vmem] * 5,
@@ -491,6 +520,7 @@
         ],
         compiler_params=params(),
     )(table, inverse, reduced, cof, named)
+    return inverse.T, precond
 
 
 def solution(mesh):

time: 40.3 us -> 35.4 us (0.88)
  local copies, waits for them, and re-layouts: 5.78 us -> 0 us
  Pallas kernels: 33.4 us -> 34.6 us
    unnamed x12 -> x0, local copies, waits for them, and re-layouts: 5.11 us -> none
    pallas_call x1, Pallas kernels: 4.75 us -> 5.81 us  [shards(): pl.pallas_call(apply_kernel, name='apply', out_shape=(jax.ShapeDtypeStruc...]
    pallas_call x1 -> x0, local copies, waits for them, and re-layouts: 0.67 us -> none  [shards(): pl.pallas_call(apply_kernel, name='apply', out_shape=(jax.ShapeDtypeStruc...]
where the time goes in v3:
time: 35.4 us; the launch traced here: 35.2 us
  Pallas kernels  34.6 us (98%)
  between operations  0.64 us (2%)
    pallas_call x1, Pallas kernels, shards(): pl.pallas_call(functools.partial(sums_kernel, devices, grps), name='sums'...  28.8 us
    pallas_call x1, Pallas kernels, shards(): pl.pallas_call(apply_kernel, name='apply', out_shape=(jax.ShapeDtypeStruc...  5.81 us

profile of v3, /device:TPU:0, one launch (start us, length us, event | category | flops | bytes accessed | tf_op | source)
XLA Modules:
  0.0 35.2 jit_solution(5236648203329598866)
XLA Ops:
  0.6 28.8 %sums.1 = (f32[9,64,128]{2,1,0:T(8,128)}, f32[16,81]{1,0:T(8,128)}, f32[32,8,128]{2,1,0:T(8,128)}, s16[512,128]{1,0:T(8,128)(2,1)}, s32[64,128]{1,0:T(8,128)}) custom-call(f32[18,8192]{1,0:T(8,128)} %cam_hbm.1, f32[6,8192]{1,0:T(8,128)} %pt_hbm.1, f32[2,8192]{1,0:T(2,128)} %res_hbm.1, s32[64,128]{1,0:T(8,128)} %bitcast.4, s32[64,128]{1,0:T(8,128)} %bitcast.5, ...), custom_call_target="tpu_custom_call" | custom-call | tf_op jit(solution)/shard_map/sums/pallas_call | solution.py:465
  29.4 5.8 %apply.1 = (f32[16,81]{1,0:T(8,128)}, f32[9,8192]{1,0:T(8,128)}) custom-call(f32[32,8,128]{2,1,0:T(8,128)} %get-tuple-element.9.table_ref, f32[16,81]{1,0:T(8,128)} %get-tuple-element.10.inv_in_ref, f32[9,64,128]{2,1,0:T(8,128)} %get-tuple-element.11.red_ref, s16[512,128]{1,0:T(8,128)(2,1)} %get-tuple-element.12.cof, s32[64,128]{1,0:T(8,128)} %get-tuple-element.13.camera_ref), custom_call_target="tpu_custom_call" | custom-call | tf_op jit(solution)/shard_map/apply/pallas_call | solution.py:503
